TPU v7x, 32 devices: a whole 2x2x4 slice. The times are simulated.
32 devices in a mesh: groups: 2 (over y), fsdp: 4 (over z), tensor: 4 (over x, core).
Axes of the slice: x: 2, y: 2, z: 4, core: 2. Of those that a mesh axis runs over, the one named last changes fastest.
Arguments:
- tokens: bfloat16 [2048, 4608], P(('groups', 'fsdp'), 'tensor'), parts along dimension 0, may hold values from -100 to 100
- norm_gain: bfloat16 [4608], P('tensor'), may hold values from 0.25 to 1.75
- w_query: bfloat16 [4608, 4096], P('fsdp', 'tensor'), may hold values from -0.5 to 0.5
- w_key: bfloat16 [4608, 2048], P('fsdp', 'tensor'), may hold values from -0.09375 to 0.09375
- w_value: bfloat16 [4608, 2048], P('fsdp', 'tensor'), may hold values from -0.09375 to 0.09375
- w_out: bfloat16 [4096, 4608], P('tensor', 'fsdp'), may hold values from -0.5 to 0.5
- post_gain: bfloat16 [4608], P('tensor'), may hold values from 0.25 to 1.75
Outputs:
- mixed: float32 [2048, 4608], P(('groups', 'fsdp'), 'tensor'), parts along dimension 0
There are 2 independent parts, one for each index of `groups`. A program takes and returns all parts, laid end to end along the dimension named above; an argument that names none is the same for every part. Nothing has to cross between parts.
All inputs are finite; a program needn't handle non-finite values.
Results may differ from a plain program's by a relative error of at most 0.0053.
Values may be sent and summed in bfloat16 or wider, within the bound.
A program may use at most 128 MiB of HBM per device.

v0:
```python
import jax
import jax.numpy as jnp
from jax import lax
from jax.sharding import PartitionSpec as P

HEAD_DIM = 128
eps_norm = 1e-06
soft_cap = 50.0
attn_scale = 144.0 ** (-0.5)
rope_base = 10000.0


def rotate(values, position):
    head_dim = values.shape[-1]
    half = head_dim // 2
    freq = rope_base ** (-(jnp.arange(half, dtype=jnp.float32) * 2.0 / head_dim))
    angle = position.astype(jnp.float32)[:, None] * freq[None, :]
    cosine = jnp.cos(angle)[:, None, :]
    sine = jnp.sin(angle)[:, None, :]
    first = values[..., :half]
    second = values[..., half:]
    return jnp.concatenate(
        [first * cosine - second * sine, second * cosine + first * sine], axis=-1
    )


def attend(query, keys, values, position):
    count, heads, head_dim = query.shape
    kv_count = keys.shape[1]
    grouped = query.reshape(count, kv_count, heads // kv_count, head_dim)
    scores = (
        jnp.einsum("nkgd,mkd->kgnm", grouped, keys, preferred_element_type=jnp.float32) * attn_scale
    )
    capped = soft_cap * jnp.tanh(scores / soft_cap)
    allowed = position[None, :] <= position[:, None]
    weights = jnp.where(allowed, jnp.exp(capped), 0.0)
    probs = (weights / jnp.sum(weights, axis=-1, keepdims=True)).astype(jnp.bfloat16)
    mixed = jnp.einsum("kgnm,mkd->nkgd", probs, values, preferred_element_type=jnp.float32)
    return mixed.reshape(count, heads * head_dim).astype(jnp.bfloat16)


def swap_pairs(n_fsdp, n_tensor, turn):
    ratio = n_fsdp // n_tensor
    pairs = []
    for f in range(n_fsdp):
        for t in range(n_tensor):
            j = (f + turn) % ratio
            pairs.append((f * n_tensor + t, (t * ratio + j) * n_tensor + f // ratio))
    return pairs


def to_rows(block, n_fsdp, n_tensor):
    rows = block.shape[0]
    ratio = n_fsdp // n_tensor
    width = block.shape[1] // ratio
    f = lax.axis_index("fsdp")
    if ratio == 1:
        held = lax.ppermute(block, ("fsdp", "tensor"), swap_pairs(n_fsdp, n_tensor, 0))
    else:
        held = jnp.zeros((ratio, rows, width), block.dtype)
        for turn in range(ratio):
            piece = lax.dynamic_slice_in_dim(block, (f + turn) % ratio * width, width, 1)
            got = lax.ppermute(piece, ("fsdp", "tensor"), swap_pairs(n_fsdp, n_tensor, turn))
            held = lax.dynamic_update_index_in_dim(held, got, (f - turn) % ratio, 0)
        held = held.reshape(ratio * rows, width)
    return lax.all_gather(held, "tensor", axis=0, tiled=True)


def from_rows(summed, rows, n_fsdp, n_tensor):
    ratio = n_fsdp // n_tensor
    width = summed.shape[1]
    f = lax.axis_index("fsdp")
    back = lambda turn: [(b, a) for a, b in swap_pairs(n_fsdp, n_tensor, turn)]
    if ratio == 1:
        return lax.ppermute(summed, ("fsdp", "tensor"), back(0))
    pieces = summed.reshape(ratio, rows, width)
    out = jnp.zeros((rows, ratio * width), summed.dtype)
    for turn in range(ratio):
        piece = lax.dynamic_index_in_dim(pieces, (f - turn) % ratio, 0, keepdims=False)
        got = lax.ppermute(piece, ("fsdp", "tensor"), back(turn))
        out = lax.dynamic_update_slice_in_dim(out, got, (f + turn) % ratio * width, 1)
    return out


def solution(mesh):
    n_fsdp, n_tensor = (mesh.shape["fsdp"], mesh.shape["tensor"])

    def on_device(tokens, norm_gain, w_query, w_key, w_value, w_out, post_gain):
        rows = tokens.shape[0]
        width = tokens.shape[1] * n_tensor
        widened = tokens.astype(jnp.float32)
        total = lax.psum(jnp.sum(widened * widened, axis=1), "tensor")
        normed = (
            widened * lax.rsqrt(total / width + eps_norm)[:, None] * norm_gain.astype(jnp.float32)
        ).astype(jnp.bfloat16)
        mine = to_rows(normed, n_fsdp, n_tensor)
        raw = []
        for piece in (w_query, w_key, w_value):
            part = jnp.dot(mine, piece, preferred_element_type=jnp.float32).astype(jnp.bfloat16)
            parts = lax.all_to_all(part, "fsdp", 0, 0, tiled=True)
            parts = parts.reshape(n_fsdp, rows, piece.shape[1])
            raw.append(jnp.sum(parts.astype(jnp.float32), axis=0))
        query_raw, key_raw, value_raw = raw
        position = jnp.arange(rows, dtype=jnp.int32)
        local_heads = w_query.shape[1] // HEAD_DIM
        local_kv = w_key.shape[1] // HEAD_DIM
        query = rotate(query_raw.reshape(rows, local_heads, HEAD_DIM), position)
        key = rotate(key_raw.reshape(rows, local_kv, HEAD_DIM), position)
        query, key = (query.astype(jnp.bfloat16), key.astype(jnp.bfloat16))
        value = value_raw.astype(jnp.bfloat16).reshape(rows, local_kv, HEAD_DIM)
        attn = attend(query, key, value, position)
        attn_all = lax.all_gather(attn, "fsdp", axis=0, tiled=True)
        part = jnp.dot(attn_all, w_out, preferred_element_type=jnp.float32).astype(jnp.bfloat16)
        summed = lax.psum_scatter(part, "tensor", scatter_dimension=0, tiled=True)
        proj = from_rows(summed, rows, n_fsdp, n_tensor).astype(jnp.float32)
        post_total = lax.psum(jnp.sum(proj * proj, axis=1), "tensor")
        branch = (
            proj * lax.rsqrt(post_total / width + eps_norm)[:, None] * post_gain.astype(jnp.float32)
        )
        return tokens.astype(jnp.float32) + branch

    placed = (
        P(("groups", "fsdp"), "tensor"),
        P("tensor"),
        P("fsdp", "tensor"),
        P("fsdp", "tensor"),
        P("fsdp", "tensor"),
        P("tensor", "fsdp"),
        P("tensor"),
    )
    return jax.shard_map(
        on_device,
        mesh=mesh,
        in_specs=placed,
        out_specs=P(("groups", "fsdp"), "tensor"),
        check_vma=False,
    )
```

profile of v0, /device:TPU:0, one launch (start us, length us, event | category | flops | bytes accessed | tf_op | source)
XLA Modules:
  0.0 329.1 jit_solution(13812048784093894810)
XLA Ops:
  6.5 0.0 copy-start
  6.5 0.0 all-gather.3.cloned.1.call-start
  6.5 1.4 fusion.2
  7.9 8.4 %psum.14 = f32[256]{0:T(256)S(1)} all-reduce(f32[256]{0:T(256)S(1)} %fusion.2), channel_id=1, replica_groups=mesh['groups'=2,'fsdp'=4,'tensor'=4] {'tensor'}, use_global_device_ids=true, to_apply=%region_1.0 | all-reduce | flops 256 | bytes 2048 | tf_op jit(solution)/shard_map/psum | solution.py:92
  16.3 0.7 convert_element_type.74
  17.0 1.3 fusion.4
  18.3 0.7 collective-permute-start
  19.0 0.0 collective-permute-done
  19.0 0.0 copy-start.3
  19.0 0.8 copy-done.3
  19.8 0.0 all-gather.3.cloned.1.call-update
  19.9 53.0 %all-gather.3.cloned.1.call-done = bf16[1024,1152]{1,0:T(8,128)(2,1)} async-done(((bf16[256,1152]{1,0:T(8,128)(2,1)}), bf16[1024,1152]{1,0:T(8,128)(2,1)}) %all-gather.3.cloned.1.call-update) | async-done | bytes 2359312 | tf_op jit(solution)/shard_map/all_gather | solution.py:66
  72.9 4.5 %convolution_convert_fusion.2 = bf16[1024,512]{1,0:T(8,128)(2,1)} fusion(bf16[1024,1152]{1,0:T(8,128)(2,1)} %all-gather.3.cloned.1.call-done, bf16[1152,512]{1,0:T(8,128)(2,1)} %param.10), kind=kOutput, calls=%fused_computation.9 | convolution fusion | flops 1208483840 | bytes 4587520 | tf_op jit(solution)/shard_map/dot_general | solution.py:99
  77.3 4.6 %all-to-all-start.1 = ((bf16[4,256,512]{2,1,0:T(8,128)(2,1)}), bf16[4,256,512]{2,1,0:T(8,128)(2,1)S(1)}, u32[]{:S(2)}, u32[]{:S(2)}) async-start(bf16[4,256,512]{2,1,0:T(8,128)(2,1)} %bitcast.36), calls=%async_computation.1 | async-start | bytes 2097152 | tf_op jit(solution)/shard_map/all_to_all | solution.py:100
  81.9 4.5 %convolution_convert_fusion.3 = bf16[1024,512]{1,0:T(8,128)(2,1)} fusion(bf16[1024,1152]{1,0:T(8,128)(2,1)} %all-gather.3.cloned.1.call-done, bf16[1152,512]{1,0:T(8,128)(2,1)} %param.11), kind=kOutput, calls=%fused_computation.10 | convolution fusion | flops 1208483840 | bytes 4587520 | tf_op jit(solution)/shard_map/dot_general | solution.py:99
  86.4 21.6 %all-to-all-done.1 = bf16[4,256,512]{2,1,0:T(8,128)(2,1)S(1)} async-done(((bf16[4,256,512]{2,1,0:T(8,128)(2,1)}), bf16[4,256,512]{2,1,0:T(8,128)(2,1)S(1)}, u32[]{:S(2)}, u32[]{:S(2)}) %all-to-all-start.1) | async-done | bytes 1048608 | tf_op jit(solution)/shard_map/all_to_all | solution.py:100
  108.1 0.0 copy-start.2
  108.1 1.0 copy-done.2
  109.0 3.5 %all-to-all-start = ((bf16[4,256,512]{2,1,0:T(8,128)(2,1)}), bf16[4,256,512]{2,1,0:T(8,128)(2,1)S(1)}, u32[]{:S(2)}, u32[]{:S(2)}) async-start(bf16[4,256,512]{2,1,0:T(8,128)(2,1)} %bitcast.35), calls=%async_computation | async-start | bytes 2097152 | tf_op jit(solution)/shard_map/all_to_all | solution.py:100
  112.6 6.6 %convolution_convert_fusion.1 = bf16[1024,1024]{1,0:T(8,128)(2,1)} fusion(bf16[1024,1152]{1,0:T(8,128)(2,1)} %all-gather.3.cloned.1.call-done, bf16[1152,1024]{1,0:T(8,128)(2,1)} %param.9), kind=kOutput, calls=%fused_computation.5 | convolution fusion | flops 2416967680 | bytes 6815744 | tf_op jit(solution)/shard_map/dot_general | solution.py:99
  119.1 18.7 %all-to-all-done = bf16[4,256,512]{2,1,0:T(8,128)(2,1)S(1)} async-done(((bf16[4,256,512]{2,1,0:T(8,128)(2,1)}), bf16[4,256,512]{2,1,0:T(8,128)(2,1)S(1)}, u32[]{:S(2)}, u32[]{:S(2)}) %all-to-all-start) | async-done | bytes 1048608 | tf_op jit(solution)/shard_map/all_to_all | solution.py:100
  137.8 4.4 %all-to-all-start.2 = ((bf16[4,256,1024]{2,1,0:T(8,128)(2,1)}), bf16[4,256,1024]{2,1,0:T(8,128)(2,1)}, u32[]{:S(2)}, u32[]{:S(2)}) async-start(bf16[4,256,1024]{2,1,0:T(8,128)(2,1)} %bitcast.33), calls=%async_computation.2 | async-start | bytes 4194304 | tf_op jit(solution)/shard_map/all_to_all | solution.py:100
  142.3 0.0 all-gather.5.cloned.1.call-start
  142.3 0.3 multiply_cosine_fusion
  142.6 0.8 copy.28
  143.4 0.8 copy.30
  144.2 0.7 iota_compare_fusion
  144.8 2.2 convert_reduce_fusion.1
  147.1 2.0 copy.26
  149.1 1.9 fusion.13
  151.0 1.9 copy.41
  152.9 2.0 copy.40
  154.9 0.9 reduce_sum.58
  155.8 1.8 copy.39
  157.6 2.2 subtract_convert_fusion.1
  159.8 30.2 %all-to-all-done.2 = bf16[4,256,1024]{2,1,0:T(8,128)(2,1)} async-done(((bf16[4,256,1024]{2,1,0:T(8,128)(2,1)}), bf16[4,256,1024]{2,1,0:T(8,128)(2,1)}, u32[]{:S(2)}, u32[]{:S(2)}) %all-to-all-start.2) | async-done | bytes 2097184 | tf_op jit(solution)/shard_map/all_to_all | solution.py:100
  190.1 2.1 convert_reduce_fusion
  192.2 1.3 copy.31
  193.5 1.3 subtract_convert_fusion
  194.8 0.3 copy.32
  195.1 1.0 copy.33
  196.1 0.0 copy-start.4
  196.1 3.6 %bitcast_select_fusion = f32[4,2,256,256]{2,3,1,0:T(8,128)} fusion(pred[256,256]{0,1:T(8,128)(4,1)} %iota_compare_fusion, bf16[256,4,2,64]{3,0,2,1:T(8,128)(2,1)} %bitcast.38, bf16[256,4,2,64]{3,0,2,1:T(8,128)(2,1)S(1)} %bitcast.37, bf16[256,4,64]{2,0,1:T(8,128)(2,1)} %get-tuple-element.6, bf16[256,4,64]{2,0,1:T(8,128)(2,1)} %get-tuple-element.5), kind=kOutput, calls=%fused_computation.2 | convolution fusion | flops 137363456 | bytes 2949120 | tf_op jit(solution)/shard_map/nkgd,mkd->kgnm/dot_general | solution.py:32
  199.7 0.0 copy-done.4
  199.7 3.5 %convolution_convert_fusion.4 = bf16[4,128,2,256]{3,1,2,0:T(8,128)(2,1)} fusion(bf16[256,4,128,1]{0,2,3,1:T(8,128)(2,1)S(1)} %bitcast.40, f32[4,2,256,256]{2,3,1,0:T(8,128)} %bitcast_select_fusion), kind=kOutput, calls=%fused_computation.13 | convolution fusion | flops 135530752 | bytes 2883584 | tf_op jit(solution)/shard_map/kgnm,mkd->nkgd/dot_general | solution.py:38
  203.2 0.0 all-gather.5.cloned.1.call-update
  203.2 0.0 reduce-scatter.2.cloned.1.call-start
  203.3 44.5 %all-gather.5.cloned.1.call-done = bf16[1024,1024]{0,1:T(8,128)(2,1)} async-done(((bf16[256,1024]{0,1:T(8,128)(2,1)}), bf16[1024,1024]{0,1:T(8,128)(2,1)}) %all-gather.5.cloned.1.call-update) | async-done | bytes 2097168 | tf_op jit(solution)/shard_map/all_gather | solution.py:112
  247.8 0.0 copy-done
  247.8 5.9 %convolution_convert_fusion = bf16[1024,1152]{1,0:T(8,128)(2,1)} fusion(bf16[1024,1024]{0,1:T(8,128)(2,1)} %all-gather.5.cloned.1.call-done, bf16[1024,1152]{1,0:T(8,128)(2,1)S(1)} %copy-done), kind=kOutput, calls=%fused_computation.1 | convolution fusion | flops 2417098752 | bytes 6815744 | tf_op jit(solution)/shard_map/dot_general | solution.py:113
  253.7 0.0 copy-start.5
  253.7 0.0 copy-start.1
  253.7 0.0 reduce-scatter.2.cloned.1.call-update
  253.7 31.1 %reduce-scatter.2.cloned.1.call-done = bf16[256,1152]{1,0:T(8,128)(2,1)} async-done(((bf16[1024,1152]{1,0:T(8,128)(2,1)}), bf16[256,1152]{1,0:T(8,128)(2,1)}) %reduce-scatter.2.cloned.1.call-update) | async-done | bytes 589840 | tf_op jit(solution)/shard_map/reduce_scatter | solution.py:114
  284.9 1.7 collective-permute-start.1
  286.6 0.0 copy-done.5
  286.6 0.0 collective-permute-done.1
  286.6 0.2 fusion
  286.8 34.6 %psum.15 = f32[256]{0:T(256)S(1)} all-reduce(f32[256]{0:T(256)S(1)} %fusion), channel_id=1, replica_groups=mesh['groups'=2,'fsdp'=4,'tensor'=4] {'tensor'}, use_global_device_ids=true, to_apply=%region_8.9 | all-reduce | flops 256 | bytes 2048 | tf_op jit(solution)/shard_map/psum | solution.py:116
  321.3 0.0 copy-done.1
  321.3 1.3 convert_add_fusion
  (5 shorter events, 0.0 us)
Async XLA Ops:
  6.5 241.2 %copy-start = (bf16[1024,1152]{1,0:T(8,128)(2,1)S(1)}, bf16[1024,1152]{1,0:T(8,128)(2,1)}, u32[]{:S(2)}) copy-start(bf16[1024,1152]{1,0:T(8,128)(2,1)} %param.12) | copy-start | bytes 7077892
  6.5 66.3 %all-gather.3.cloned.1.call-start = ((), (), s32[]{:S(2)}) async-start(), calls=%async_computation.4 | async-start | bytes 2949120 | tf_op jit(solution)/shard_map/all_gather | solution.py:66
  18.3 0.7 collective-permute-start
  19.0 0.8 copy-start.3
  77.3 30.7 %all-to-all-start.1 = ((bf16[4,256,512]{2,1,0:T(8,128)(2,1)}), bf16[4,256,512]{2,1,0:T(8,128)(2,1)S(1)}, u32[]{:S(2)}, u32[]{:S(2)}) async-start(bf16[4,256,512]{2,1,0:T(8,128)(2,1)} %bitcast.36), calls=%async_computation.1 | async-start | bytes 2097152 | tf_op jit(solution)/shard_map/all_to_all | solution.py:100
  108.1 1.0 copy-start.2
  109.0 28.8 %all-to-all-start = ((bf16[4,256,512]{2,1,0:T(8,128)(2,1)}), bf16[4,256,512]{2,1,0:T(8,128)(2,1)S(1)}, u32[]{:S(2)}, u32[]{:S(2)}) async-start(bf16[4,256,512]{2,1,0:T(8,128)(2,1)} %bitcast.35), calls=%async_computation | async-start | bytes 2097152 | tf_op jit(solution)/shard_map/all_to_all | solution.py:100
  137.8 52.3 %all-to-all-start.2 = ((bf16[4,256,1024]{2,1,0:T(8,128)(2,1)}), bf16[4,256,1024]{2,1,0:T(8,128)(2,1)}, u32[]{:S(2)}, u32[]{:S(2)}) async-start(bf16[4,256,1024]{2,1,0:T(8,128)(2,1)} %bitcast.33), calls=%async_computation.2 | async-start | bytes 4194304 | tf_op jit(solution)/shard_map/all_to_all | solution.py:100
  142.3 105.5 %all-gather.5.cloned.1.call-start = ((), (), s32[]{:S(2)}) async-start(), calls=%async_computation.5 | async-start | bytes 2621440 | tf_op jit(solution)/shard_map/all_gather | solution.py:112
  196.1 3.6 %copy-start.4 = (bf16[256,512]{0,1:T(8,128)(2,1)S(1)}, bf16[256,512]{0,1:T(8,128)(2,1)}, u32[]{:S(2)}) copy-start(bf16[256,512]{0,1:T(8,128)(2,1)} %copy.39) | copy-start | bytes 786436
  203.2 81.7 %reduce-scatter.2.cloned.1.call-start = ((), (), s32[]{:S(2)}) async-start(), calls=%async_computation.6 | async-start | bytes 2949120 | tf_op jit(solution)/shard_map/reduce_scatter | solution.py:114
  253.7 32.9 %copy-start.5 = (bf16[1152]{0:T(1024)(128)(2,1)S(1)}, bf16[1152]{0:T(1024)(128)(2,1)}, u32[]{:S(2)}) copy-start(bf16[1152]{0:T(1024)(128)(2,1)} %param.13) | copy-start | bytes 6916
  253.7 67.7 %copy-start.1 = (bf16[256,1152]{1,0:T(8,128)(2,1)S(1)}, bf16[256,1152]{1,0:T(8,128)(2,1)}, u32[]{:S(2)}) copy-start(bf16[256,1152]{1,0:T(8,128)(2,1)} %param.7) | copy-start | bytes 1769476
  284.9 1.7 collective-permute-start.1
Sparse Core Ops, SparseCore 0:
  20.0 52.8 all-gather.2
  203.3 44.3 all-gather.4
  253.8 30.9 reduce-scatter.1
where the time goes:
time: 330 us; the launch traced here: 329 us
  waiting for transfers between devices  199 us (60%)
  blocking collectives  42.9 us (13%)
  matrix products  28.5 us (9%)
  local copies, waits for them, and re-layouts  15.6 us (5%)
  starting transfers between devices  15 us (5%)
  other arithmetic  14.6 us (4%)
  between operations  13.2 us (4%)
    all_to_all x3, waiting for transfers between devices, on_device(): parts = lax.all_to_all(part, 'fsdp', 0, 0, tiled=True)  70.5 us
    all_gather x1, waiting for transfers between devices, to_rows(): return lax.all_gather(held, 'tensor', axis=0, tiled=True)  53 us
    all_gather x1, waiting for transfers between devices, on_device(): attn_all = lax.all_gather(attn, 'fsdp', axis=0, tiled=True)  44.5 us
    psum x1, blocking collectives, on_device(): post_total = lax.psum(jnp.sum(proj * proj, axis=1), 'tensor')  34.6 us
    reduce_scatter x1, waiting for transfers between devices, on_device(): summed = lax.psum_scatter(part, 'tensor', scatter_dimension=0, tiled=True)  31.1 us
    dot_general x3, matrix products, on_device(): jnp.dot(mine, piece, preferred_element_type=jnp.float32)  15.5 us
    all_to_all x3, starting transfers between devices, on_device(): parts = lax.all_to_all(part, 'fsdp', 0, 0, tiled=True)  12.6 us
    psum x1, blocking collectives, on_device(): total = lax.psum(jnp.sum(widened * widened, axis=1), 'tensor')  8.37 us
  transfers between devices with their start and end apart: 8, of which 6 were waited for; matrix products, arithmetic and copies ran while one was open for 9% of the time, Pallas kernels for 0%

commit v1 on v0

--- a/solution.py
+++ b/solution.py
@@ -63,7 +63,9 @@
             got = lax.ppermute(piece, ("fsdp", "tensor"), swap_pairs(n_fsdp, n_tensor, turn))
             held = lax.dynamic_update_index_in_dim(held, got, (f - turn) % ratio, 0)
         held = held.reshape(ratio * rows, width)
-    return lax.all_gather(held, "tensor", axis=0, tiled=True)
+    return jnp.concatenate(
+        lax.all_to_all(jnp.stack([held] * lax.axis_size("tensor")), "tensor", 0, 0), axis=0
+    )
 
 
 def from_rows(summed, rows, n_fsdp, n_tensor):

time: 330 us -> 335 us (1.015)
  blocking collectives: 42.9 us -> 104 us
  waiting for transfers between devices: 199 us -> 146 us
    all_to_all x0 -> x1, blocking collectives: none -> 61.5 us  [to_rows(): lax.all_to_all(jnp.stack([held] * lax.axis_size('tensor')), 'tensor', 0, 0)]
    all_gather x1 -> x0, waiting for transfers between devices: 53 us -> none  [to_rows(): return lax.all_gather(held, 'tensor', axis=0, tiled=True)]
  transfers between devices with their start and end apart: 8 -> 7, of which waited for: 6 -> 5; matrix products, arithmetic and copies ran while one was open for 9% -> 9% of each run, Pallas kernels for 0% -> 0%
where the time goes in v1:
time: 335 us; the launch traced here: 334 us
  waiting for transfers between devices  146 us (44%)
  blocking collectives  104 us (31%)
  matrix products  26.5 us (8%)
  local copies, waits for them, and re-layouts  14.9 us (4%)
  other arithmetic  14.6 us (4%)
  starting transfers between devices  14 us (4%)
  between operations  13.5 us (4%)
    all_to_all x3, waiting for transfers between devices, on_device(): parts = lax.all_to_all(part, 'fsdp', 0, 0, tiled=True)  70.1 us
    all_to_all x1, blocking collectives, to_rows(): lax.all_to_all(jnp.stack([held] * lax.axis_size('tensor')), 'tensor', 0, 0)  61.5 us
    all_gather x1, waiting for transfers between devices, on_device(): attn_all = lax.all_gather(attn, 'fsdp', axis=0, tiled=True)  44.8 us
    psum x1, blocking collectives, on_device(): post_total = lax.psum(jnp.sum(proj * proj, axis=1), 'tensor')  34.6 us
    reduce_scatter x1, waiting for transfers between devices, on_device(): summed = lax.psum_scatter(part, 'tensor', scatter_dimension=0, tiled=True)  31.1 us
    dot_general x3, matrix products, on_device(): jnp.dot(mine, piece, preferred_element_type=jnp.float32)  13.5 us
    all_to_all x3, starting transfers between devices, on_device(): parts = lax.all_to_all(part, 'fsdp', 0, 0, tiled=True)  11.5 us
    psum x1, blocking collectives, on_device(): total = lax.psum(jnp.sum(widened * widened, axis=1), 'tensor')  8.37 us
  transfers between devices with their start and end apart: 7, of which 5 were waited for; matrix products, arithmetic and copies ran while one was open for 9% of the time, Pallas kernels for 0%

profile of v1, /device:TPU:0, one launch (start us, length us, event | category | flops | bytes accessed | tf_op | source)
XLA Modules:
  0.0 334.1 jit_solution(2577082363246909949)
XLA Ops:
  6.5 0.0 copy-start
  6.5 1.4 fusion.2
  7.9 8.4 %psum.14 = f32[256]{0:T(256)S(1)} all-reduce(f32[256]{0:T(256)S(1)} %fusion.2), channel_id=1, replica_groups=mesh['groups'=2,'fsdp'=4,'tensor'=4] {'tensor'}, use_global_device_ids=true, to_apply=%region_1.0 | all-reduce | flops 256 | bytes 2048 | tf_op jit(solution)/shard_map/psum | solution.py:94
  16.3 0.7 convert_element_type.74
  17.0 1.3 fusion.4
  18.3 0.7 collective-permute-start
  19.0 0.0 collective-permute-done
  19.0 0.2 stack.2
  19.2 0.0 copy-start.6
  19.2 61.5 %all_to_all.32 = bf16[4,256,1152]{2,1,0:T(8,128)(2,1)S(1)} all-to-all(bf16[4,256,1152]{2,1,0:T(8,128)(2,1)S(1)} %stack.2), channel_id=1, replica_groups=mesh['groups'=2,'fsdp'=4,'tensor'=4] {'tensor'}, dimensions={0} | all-to-all | bytes 4718592 | tf_op jit(solution)/shard_map/all_to_all | solution.py:67
  80.7 0.0 copy-start.3
  80.7 0.0 copy-done.6
  80.7 2.5 convolution_convert_fusion.2
  83.2 0.0 copy-done.3
  83.2 3.5 %all-to-all-start.2 = ((bf16[4,256,512]{2,1,0:T(8,128)(2,1)}), bf16[4,256,512]{2,1,0:T(8,128)(2,1)S(1)}, u32[]{:S(2)}, u32[]{:S(2)}) async-start(bf16[4,256,512]{2,1,0:T(8,128)(2,1)} %bitcast.40), calls=%async_computation.2 | async-start | bytes 2097152 | tf_op jit(solution)/shard_map/all_to_all | solution.py:102
  86.7 4.5 %convolution_convert_fusion.3 = bf16[1024,512]{1,0:T(8,128)(2,1)} fusion(bf16[1024,1152]{1,0:T(8,128)(2,1)} %bitcast.35, bf16[1152,512]{1,0:T(8,128)(2,1)} %param.11), kind=kOutput, calls=%fused_computation.10 | convolution fusion | flops 1208483840 | bytes 4587520 | tf_op jit(solution)/shard_map/dot_general | solution.py:101
  91.2 21.1 %all-to-all-done.2 = bf16[4,256,512]{2,1,0:T(8,128)(2,1)S(1)} async-done(((bf16[4,256,512]{2,1,0:T(8,128)(2,1)}), bf16[4,256,512]{2,1,0:T(8,128)(2,1)S(1)}, u32[]{:S(2)}, u32[]{:S(2)}) %all-to-all-start.2) | async-done | bytes 1048608 | tf_op jit(solution)/shard_map/all_to_all | solution.py:102
  112.3 0.0 copy-start.2
  112.3 1.0 copy-done.2
  113.3 3.5 %all-to-all-start.1 = ((bf16[4,256,512]{2,1,0:T(8,128)(2,1)}), bf16[4,256,512]{2,1,0:T(8,128)(2,1)S(1)}, u32[]{:S(2)}, u32[]{:S(2)}) async-start(bf16[4,256,512]{2,1,0:T(8,128)(2,1)} %bitcast.39), calls=%async_computation.1 | async-start | bytes 2097152 | tf_op jit(solution)/shard_map/all_to_all | solution.py:102
  116.8 6.6 %convolution_convert_fusion.1 = bf16[1024,1024]{1,0:T(8,128)(2,1)} fusion(bf16[1024,1152]{1,0:T(8,128)(2,1)} %bitcast.36, bf16[1152,1024]{1,0:T(8,128)(2,1)} %param.9), kind=kOutput, calls=%fused_computation.5 | convolution fusion | flops 2416967680 | bytes 6815744 | tf_op jit(solution)/shard_map/dot_general | solution.py:101
  123.4 18.7 %all-to-all-done.1 = bf16[4,256,512]{2,1,0:T(8,128)(2,1)S(1)} async-done(((bf16[4,256,512]{2,1,0:T(8,128)(2,1)}), bf16[4,256,512]{2,1,0:T(8,128)(2,1)S(1)}, u32[]{:S(2)}, u32[]{:S(2)}) %all-to-all-start.1) | async-done | bytes 1048608 | tf_op jit(solution)/shard_map/all_to_all | solution.py:102
  142.1 4.4 %all-to-all-start.3 = ((bf16[4,256,1024]{2,1,0:T(8,128)(2,1)}), bf16[4,256,1024]{2,1,0:T(8,128)(2,1)}, u32[]{:S(2)}, u32[]{:S(2)}) async-start(bf16[4,256,1024]{2,1,0:T(8,128)(2,1)} %bitcast.37), calls=%async_computation.3 | async-start | bytes 4194304 | tf_op jit(solution)/shard_map/all_to_all | solution.py:102
  146.5 0.0 all-gather.2.cloned.1.call-start
  146.6 0.3 multiply_cosine_fusion
  146.9 0.8 copy.28
  147.7 0.8 copy.30
  148.4 0.6 iota_compare_fusion
  149.1 2.2 convert_reduce_fusion.1
  151.3 2.0 copy.26
  153.3 1.9 fusion.13
  155.2 1.9 copy.41
  157.2 1.9 copy.40
  159.1 0.9 reduce_sum.58
  160.0 1.8 copy.39
  161.9 2.2 subtract_convert_fusion.1
  164.1 30.3 %all-to-all-done.3 = bf16[4,256,1024]{2,1,0:T(8,128)(2,1)} async-done(((bf16[4,256,1024]{2,1,0:T(8,128)(2,1)}), bf16[4,256,1024]{2,1,0:T(8,128)(2,1)}, u32[]{:S(2)}, u32[]{:S(2)}) %all-to-all-start.3) | async-done | bytes 2097184 | tf_op jit(solution)/shard_map/all_to_all | solution.py:102
  194.3 2.1 convert_reduce_fusion
  196.4 1.3 copy.31
  197.7 1.3 subtract_convert_fusion
  199.1 0.3 copy.32
  199.4 1.0 copy.33
  200.4 0.0 copy-start.4
  200.4 3.6 %bitcast_select_fusion = f32[4,2,256,256]{2,3,1,0:T(8,128)} fusion(pred[256,256]{0,1:T(8,128)(4,1)} %iota_compare_fusion, bf16[256,4,2,64]{3,0,2,1:T(8,128)(2,1)} %bitcast.42, bf16[256,4,2,64]{3,0,2,1:T(8,128)(2,1)S(1)} %bitcast.41, bf16[256,4,64]{2,0,1:T(8,128)(2,1)} %get-tuple-element.6, bf16[256,4,64]{2,0,1:T(8,128)(2,1)} %get-tuple-element.5), kind=kOutput, calls=%fused_computation.2 | convolution fusion | flops 137363456 | bytes 2949120 | tf_op jit(solution)/shard_map/nkgd,mkd->kgnm/dot_general | solution.py:32
  204.0 0.0 copy-done.4
  204.0 3.5 %convolution_convert_fusion.4 = bf16[4,128,2,256]{3,1,2,0:T(8,128)(2,1)} fusion(bf16[256,4,128,1]{0,2,3,1:T(8,128)(2,1)S(1)} %bitcast.44, f32[4,2,256,256]{2,3,1,0:T(8,128)} %bitcast_select_fusion), kind=kOutput, calls=%fused_computation.13 | convolution fusion | flops 135530752 | bytes 2883584 | tf_op jit(solution)/shard_map/kgnm,mkd->nkgd/dot_general | solution.py:38
  207.5 0.0 all-gather.2.cloned.1.call-update
  207.5 0.0 reduce-scatter.2.cloned.1.call-start
  207.5 44.8 %all-gather.2.cloned.1.call-done = bf16[1024,1024]{0,1:T(8,128)(2,1)} async-done(((bf16[256,1024]{0,1:T(8,128)(2,1)}), bf16[1024,1024]{0,1:T(8,128)(2,1)}) %all-gather.2.cloned.1.call-update) | async-done | bytes 2097168 | tf_op jit(solution)/shard_map/all_gather | solution.py:114
  252.4 0.0 copy-done
  252.4 5.9 %convolution_convert_fusion = bf16[1024,1152]{1,0:T(8,128)(2,1)} fusion(bf16[1024,1024]{0,1:T(8,128)(2,1)} %all-gather.2.cloned.1.call-done, bf16[1024,1152]{1,0:T(8,128)(2,1)S(1)} %copy-done), kind=kOutput, calls=%fused_computation.1 | convolution fusion | flops 2417098752 | bytes 6815744 | tf_op jit(solution)/shard_map/dot_general | solution.py:115
  258.3 0.0 copy-start.5
  258.3 0.0 copy-start.1
  258.3 0.0 reduce-scatter.2.cloned.1.call-update
  258.3 31.1 %reduce-scatter.2.cloned.1.call-done = bf16[256,1152]{1,0:T(8,128)(2,1)} async-done(((bf16[1024,1152]{1,0:T(8,128)(2,1)}), bf16[256,1152]{1,0:T(8,128)(2,1)}) %reduce-scatter.2.cloned.1.call-update) | async-done | bytes 589840 | tf_op jit(solution)/shard_map/reduce_scatter | solution.py:116
  289.5 1.7 collective-permute-start.1
  291.2 0.0 copy-done.5
  291.2 0.0 collective-permute-done.1
  291.2 0.2 fusion
  291.4 34.6 %psum.15 = f32[256]{0:T(256)S(1)} all-reduce(f32[256]{0:T(256)S(1)} %fusion), channel_id=1, replica_groups=mesh['groups'=2,'fsdp'=4,'tensor'=4] {'tensor'}, use_global_device_ids=true, to_apply=%region_8.9 | all-reduce | flops 256 | bytes 2048 | tf_op jit(solution)/shard_map/psum | solution.py:118
  326.0 0.0 copy-done.1
  326.0 1.3 convert_add_fusion
  (5 shorter events, 0.0 us)
Async XLA Ops:
  6.5 245.8 %copy-start = (bf16[1024,1152]{1,0:T(8,128)(2,1)S(1)}, bf16[1024,1152]{1,0:T(8,128)(2,1)}, u32[]{:S(2)}) copy-start(bf16[1024,1152]{1,0:T(8,128)(2,1)} %param.12) | copy-start | bytes 7077892
  18.3 0.7 collective-permute-start
  19.2 61.5 %copy-start.6 = (bf16[1152,512]{1,0:T(8,128)(2,1)S(1)}, bf16[1152,512]{1,0:T(8,128)(2,1)}, u32[]{:S(2)}) copy-start(bf16[1152,512]{1,0:T(8,128)(2,1)} %param.10) | copy-start | bytes 3538948
  80.7 2.5 copy-start.3
  83.2 29.1 %all-to-all-start.2 = ((bf16[4,256,512]{2,1,0:T(8,128)(2,1)}), bf16[4,256,512]{2,1,0:T(8,128)(2,1)S(1)}, u32[]{:S(2)}, u32[]{:S(2)}) async-start(bf16[4,256,512]{2,1,0:T(8,128)(2,1)} %bitcast.40), calls=%async_computation.2 | async-start | bytes 2097152 | tf_op jit(solution)/shard_map/all_to_all | solution.py:102
  112.3 1.0 copy-start.2
  113.3 28.8 %all-to-all-start.1 = ((bf16[4,256,512]{2,1,0:T(8,128)(2,1)}), bf16[4,256,512]{2,1,0:T(8,128)(2,1)S(1)}, u32[]{:S(2)}, u32[]{:S(2)}) async-start(bf16[4,256,512]{2,1,0:T(8,128)(2,1)} %bitcast.39), calls=%async_computation.1 | async-start | bytes 2097152 | tf_op jit(solution)/shard_map/all_to_all | solution.py:102
  142.1 52.3 %all-to-all-start.3 = ((bf16[4,256,1024]{2,1,0:T(8,128)(2,1)}), bf16[4,256,1024]{2,1,0:T(8,128)(2,1)}, u32[]{:S(2)}, u32[]{:S(2)}) async-start(bf16[4,256,1024]{2,1,0:T(8,128)(2,1)} %bitcast.37), calls=%async_computation.3 | async-start | bytes 4194304 | tf_op jit(solution)/shard_map/all_to_all | solution.py:102
  146.5 105.8 %all-gather.2.cloned.1.call-start = ((), (), s32[]{:S(2)}) async-start(), calls=%async_computation.5 | async-start | bytes 2621440 | tf_op jit(solution)/shard_map/all_gather | solution.py:114
  200.4 3.6 %copy-start.4 = (bf16[256,512]{0,1:T(8,128)(2,1)S(1)}, bf16[256,512]{0,1:T(8,128)(2,1)}, u32[]{:S(2)}) copy-start(bf16[256,512]{0,1:T(8,128)(2,1)} %copy.39) | copy-start | bytes 786436
  207.5 82.0 %reduce-scatter.2.cloned.1.call-start = ((), (), s32[]{:S(2)}) async-start(), calls=%async_computation.6 | async-start | bytes 2949120 | tf_op jit(solution)/shard_map/reduce_scatter | solution.py:116
  258.3 32.9 %copy-start.5 = (bf16[1152]{0:T(1024)(128)(2,1)S(1)}, bf16[1152]{0:T(1024)(128)(2,1)}, u32[]{:S(2)}) copy-start(bf16[1152]{0:T(1024)(128)(2,1)} %param.13) | copy-start | bytes 6916
  258.3 67.7 %copy-start.1 = (bf16[256,1152]{1,0:T(8,128)(2,1)S(1)}, bf16[256,1152]{1,0:T(8,128)(2,1)}, u32[]{:S(2)}) copy-start(bf16[256,1152]{1,0:T(8,128)(2,1)} %param.7) | copy-start | bytes 1769476
  289.5 1.7 collective-permute-start.1
Sparse Core Ops, SparseCore 0:
  207.6 44.7 all-gather.1
  258.4 30.9 reduce-scatter.1
